TPU v7x, 32 devices: a whole 2x2x4 slice. The times are simulated.
32 devices in a mesh: lat: 4 (over y, x), lon: 8 (over z, core).
Axes of the slice: x: 2, y: 2, z: 4, core: 2. Of those that a mesh axis runs over, the one named last changes fastest.
Arguments:
- forcing: float32 [256, 2048], P('lat', 'lon'), may hold values from -32 to 32
- depth_east: float32 [256, 2048], P('lat', 'lon'), may hold values from 0.25 to 4
- depth_north: float32 [256, 2048], P('lat', 'lon'), may hold values from 0.25 to 4
- surface_term: float32 [256, 2048], P('lat', 'lon'), may hold values from 0.02 to 0.5
- ocean_mask: int32 [256, 2048], P('lat', 'lon'), may hold values 0 or 1
- cost_weights: float32 [8, 256, 2048], P(None, 'lat', 'lon'), may hold values from -6 to 6
Outputs:
- forcing_adjoint: float32 [8, 256, 2048], P(None, 'lat', 'lon')
- east_gradient: float32 [8, 256, 2048], P(None, 'lat', 'lon')
- north_gradient: float32 [8, 256, 2048], P(None, 'lat', 'lon')
Inputs may be any that keep to these rules, and one draw needn't show every extreme that they name: `ocean_mask`: 1 marks an ocean cell, 0 a land cell.
All inputs are finite; a program needn't handle non-finite values. No bound on the sum of `ocean_mask` on one device may be relied on, other than what follows from the above.
Results may differ from a plain program's by a relative error of at most 0.00018.
Values sent between devices are 32-bit elements; how exact they have to be, the bound alone decides.
A program may use at most 64 MiB of HBM per device.

v0:
```python
import jax
import jax.numpy as jnp
from jax import lax
from jax.sharding import PartitionSpec as P

ITERS = 6


def padded_2(block, sides, width, periodic):
    for axis, dim in sides:
        count = lax.axis_size(axis)
        forward = [(i, i + 1) for i in range(count - 1)]
        if periodic:
            forward.append((count - 1, 0))
        backward = [(target, source) for source, target in forward]
        low = lax.ppermute(
            lax.slice_in_dim(block, block.shape[dim] - width, None, axis=dim), axis, forward
        )
        high = lax.ppermute(lax.slice_in_dim(block, 0, width, axis=dim), axis, backward)
        block = jnp.concatenate([low, block, high], axis=dim)
    return block


def shifted(value, axis, steps):
    count = lax.axis_size(axis)
    pairs = [(source, (source + steps) % count) for source in range(count)]
    return lax.ppermute(value, axis, pairs)


def shifted_2(block, axis, distance):
    devices = range(lax.axis_size(axis))
    route = [(i - distance, i) for i in devices if i - distance in devices]
    return lax.ppermute(block, axis, route)


def widen_coefs(stacked):
    wider = padded_2(stacked, (("lon", 2),), 1, True)
    return padded_2(wider, (("lat", 1),), 1, False)


def widen_precond(field):
    wider = padded_2(field, (("lon", 1),), 1, True)
    return padded_2(wider, (("lat", 0),), 1, False)


def widen_image(stack):
    wider = padded_2(stack, (("lon", 2),), 1, True)
    return padded_2(wider, (("lat", 1),), 1, False)


def operate(padded, coefs):
    base, east_face, west_face, north_face, south_face = coefs
    centre = padded[..., 1:-1, 1:-1]
    return (
        base * centre
        + east_face * (centre - padded[..., 1:-1, 2:])
        + west_face * (centre - padded[..., 1:-1, :-2])
        + north_face * (centre - padded[..., 2:, 1:-1])
        + south_face * (centre - padded[..., :-2, 1:-1])
    )


def smoothed_terms(residual, diagonal, coefs):
    precond = residual / diagonal
    prec_pad = widen_precond(precond)
    smooth = operate(prec_pad, coefs)
    norm_value, delta = lax.psum(
        (jnp.sum(residual * precond), jnp.sum(precond * smooth)), ("lat", "lon")
    )
    return (prec_pad, smooth, norm_value, delta)


def body(forcing, depth_east, depth_north, surface_term, ocean_mask, cost_weights):
    stacked = jnp.stack([ocean_mask.astype(jnp.float32), depth_east, depth_north])
    padded = widen_coefs(stacked)
    wet = padded[0]
    east_all = padded[1][:, :-1] * wet[:, :-1] * wet[:, 1:]
    north_all = padded[2][:-1, :] * wet[:-1, :] * wet[1:, :]
    east_face = east_all[1:-1, 1:]
    west_face = east_all[1:-1, :-1]
    north_face = north_all[1:, 1:-1]
    south_face = north_all[:-1, 1:-1]
    ocean = wet[1:-1, 1:-1]
    mask_east = ocean * wet[1:-1, 2:]
    mask_north = ocean * wet[2:, 1:-1]
    base = ocean * surface_term + 1.0 - ocean
    diagonal = base + east_face + west_face + north_face + south_face
    coefs = (base, east_face, west_face, north_face, south_face)
    residual = forcing
    padded_dirs = []
    images = []
    residuals = []
    alphas = []
    betas = []
    pairs = []
    prec_pad, smooth, norm_first, delta = smoothed_terms(residual, diagonal, coefs)
    norms = [norm_first]
    alpha = norm_first / delta
    dir_pad = prec_pad
    image = smooth
    for step in range(ITERS):
        padded_dirs.append(dir_pad)
        images.append(image)
        alphas.append(alpha)
        pairs.append(norms[-1] / alpha)
        residual = residual - alpha * image
        if step < ITERS - 1:
            residuals.append(residual)
            prec_pad, smooth, norm_next, delta = smoothed_terms(residual, diagonal, coefs)
            beta = norm_next / norms[-1]
            alpha = norm_next / (delta - beta * norm_next / alpha)
            dir_pad = prec_pad + beta * dir_pad
            image = smooth + beta * image
            norms.append(norm_next)
            betas.append(beta)
    projections = lax.psum(
        jnp.stack(
            [
                jnp.sum(cost_weights * padded_dirs[step][1:-1, 1:-1], axis=(1, 2))
                for step in range(ITERS)
            ]
        ),
        ("lat", "lon"),
    )
    last = ITERS - 1
    dir_pad = padded_dirs[last]
    inner_dir = dir_pad[1:-1, 1:-1]
    alpha_bar = projections[last]
    norm_bar = alpha_bar / pairs[last]
    pair_bar = -alpha_bar * alphas[last] / pairs[last]
    scale = pair_bar[:, None, None]
    dir_bar = alphas[last] * cost_weights + 2.0 * scale * images[last]
    east_diff = inner_dir - dir_pad[1:-1, 2:]
    north_diff = inner_dir - dir_pad[2:, 1:-1]
    east_sum = scale * (east_diff * east_diff)
    north_sum = scale * (north_diff * north_diff)
    res_bar = jnp.zeros_like(cost_weights)
    depth_bar = jnp.zeros_like(cost_weights)
    for step in range(ITERS - 2, -1, -1):
        dir_pad = padded_dirs[step]
        inner_dir = dir_pad[1:-1, 1:-1]
        image = images[step]
        resid_next = residuals[step]
        precond_next = resid_next / diagonal
        scaled = dir_bar / diagonal
        beta_term = lax.psum(jnp.sum(dir_bar * inner_dir, axis=(1, 2)), ("lat", "lon"))
        norm_next_bar = norm_bar + beta_term / norms[step]
        res_new = res_bar + scaled + 2.0 * norm_next_bar[:, None, None] * precond_next
        alpha_bar = projections[step] - lax.psum(
            jnp.sum(res_new * image, axis=(1, 2)), ("lat", "lon")
        )
        pre_bar = dir_bar + norm_next_bar[:, None, None] * resid_next
        depth_bar = depth_bar - pre_bar * precond_next / diagonal
        norm_bar = (
            -beta_term * norms[step + 1] / (norms[step] * norms[step]) + alpha_bar / pairs[step]
        )
        pair_bar = -alpha_bar * alphas[step] / pairs[step]
        scale = pair_bar[:, None, None]
        image_pad = widen_image(-alphas[step] * res_new + scale * inner_dir)
        dir_bar = (
            betas[step] * dir_bar
            + alphas[step] * cost_weights
            + scale * image
            + operate(image_pad, coefs)
        )
        centre = image_pad[:, 1:-1, 1:-1]
        east_sum = east_sum + (centre - image_pad[:, 1:-1, 2:]) * (inner_dir - dir_pad[1:-1, 2:])
        north_sum = north_sum + (centre - image_pad[:, 2:, 1:-1]) * (inner_dir - dir_pad[2:, 1:-1])
        res_bar = res_new
    precond_first = forcing / diagonal
    pre_bar = dir_bar + norm_bar[:, None, None] * forcing
    forcing_adjoint = res_bar + dir_bar / diagonal + 2.0 * norm_bar[:, None, None] * precond_first
    depth_bar = depth_bar - pre_bar * precond_first / diagonal
    east_column = shifted(depth_bar[:, :, :1], "lon", -1)
    north_row = shifted_2(depth_bar[:, :1, :], "lat", -1)
    depth_eastward = jnp.concatenate([depth_bar[:, :, 1:], east_column], axis=2)
    depth_northward = jnp.concatenate([depth_bar[:, 1:, :], north_row], axis=1)
    east_gradient = mask_east * (east_sum + depth_bar + depth_eastward)
    north_gradient = mask_north * (north_sum + depth_bar + depth_northward)
    return (forcing_adjoint, east_gradient, north_gradient)


def solution(mesh):
    return jax.shard_map(
        body,
        mesh=mesh,
        in_specs=(
            P("lat", "lon"),
            P("lat", "lon"),
            P("lat", "lon"),
            P("lat", "lon"),
            P("lat", "lon"),
            P(None, "lat", "lon"),
        ),
        out_specs=(P(None, "lat", "lon"), P(None, "lat", "lon"), P(None, "lat", "lon")),
        check_vma=False,
    )
```

profile of v0, /device:TPU:31, one launch (start us, length us, event | category | flops | bytes accessed | tf_op | source)
XLA Modules:
  0.0 978.9 jit_solution(14568244211439639987)
XLA Ops:
  3.8 4.2 collective-permute-done.1
  9.4 4.0 collective-permute-start.3
  16.2 3.5 collective-permute-start.5
  21.5 3.6 collective-permute-start.6
  26.4 3.6 collective-permute-done.7
  30.8 41.1 %all-reduce.5 = (f32[]{:T(128)}, f32[]{:T(128)}) all-reduce(f32[]{:T(128)} %get-tuple-element.20, f32[]{:T(128)} %get-tuple-element.19), channel_id=1, replica_groups=mesh['lat'=4,'lon'=8] {'lat','lon'}, use_global_device_ids=true, to_apply=%region_1.0 | all-reduce | flops 2 | bytes 16 | tf_op jit(solution)/shard_map/psum | solution.py:67
  73.4 2.9 collective-permute-start.8
  79.1 3.2 collective-permute-start.10
  83.6 3.0 collective-permute-done.11
  87.5 41.0 %all-reduce.4 = (f32[]{:T(128)}, f32[]{:T(128)}) all-reduce(f32[]{:T(128)} %get-tuple-element.18, f32[]{:T(128)} %get-tuple-element.17), channel_id=1, replica_groups=mesh['lat'=4,'lon'=8] {'lat','lon'}, use_global_device_ids=true, to_apply=%region_5.0 | all-reduce | flops 2 | bytes 16 | tf_op jit(solution)/shard_map/psum | solution.py:67
  133.1 2.9 collective-permute-start.12
  138.8 3.1 collective-permute-start.14
  143.2 3.0 collective-permute-done.15
  147.0 40.9 %all-reduce.3 = (f32[]{:T(128)}, f32[]{:T(128)}) all-reduce(f32[]{:T(128)} %get-tuple-element.16, f32[]{:T(128)} %get-tuple-element.15), channel_id=1, replica_groups=mesh['lat'=4,'lon'=8] {'lat','lon'}, use_global_device_ids=true, to_apply=%region_9.0 | all-reduce | flops 2 | bytes 16 | tf_op jit(solution)/shard_map/psum | solution.py:67
  192.0 2.9 collective-permute-start.16
  197.6 3.1 collective-permute-start.18
  202.1 3.0 collective-permute-done.19
  205.9 40.9 %all-reduce.2 = (f32[]{:T(128)}, f32[]{:T(128)}) all-reduce(f32[]{:T(128)} %get-tuple-element.14, f32[]{:T(128)} %get-tuple-element.13), channel_id=1, replica_groups=mesh['lat'=4,'lon'=8] {'lat','lon'}, use_global_device_ids=true, to_apply=%region_13.0 | all-reduce | flops 2 | bytes 16 | tf_op jit(solution)/shard_map/psum | solution.py:67
  250.7 2.9 collective-permute-start.20
  256.6 3.0 collective-permute-start.22
  260.9 3.0 collective-permute-done.23
  264.7 40.9 %all-reduce.1 = (f32[]{:T(128)}, f32[]{:T(128)}) all-reduce(f32[]{:T(128)} %get-tuple-element.12, f32[]{:T(128)} %get-tuple-element.11), channel_id=1, replica_groups=mesh['lat'=4,'lon'=8] {'lat','lon'}, use_global_device_ids=true, to_apply=%region_17.0 | all-reduce | flops 2 | bytes 16 | tf_op jit(solution)/shard_map/psum | solution.py:67
  309.4 2.9 collective-permute-start.24
  315.1 3.1 collective-permute-start.26
  320.1 2.4 collective-permute-done.27
  323.3 41.0 %psum.171 = f32[]{:T(128)} all-reduce(f32[]{:T(128)} %get-tuple-element.10), channel_id=1, replica_groups=mesh['lat'=4,'lon'=8] {'lat','lon'}, use_global_device_ids=true, to_apply=%region_21.0 | all-reduce | flops 1 | bytes 8 | tf_op jit(solution)/shard_map/psum | solution.py:67
  370.4 42.2 %all-reduce = (f32[6,8]{1,0:T(8,128)S(1)}, f32[]{:T(128)}) all-reduce(f32[6,8]{1,0:T(8,128)S(1)} %stack.43, f32[]{:T(128)} %get-tuple-element.9), channel_id=1, replica_groups=mesh['lat'=4,'lon'=8] {'lat','lon'}, use_global_device_ids=true, to_apply=%region_30.0 | all-reduce | flops 49 | bytes 392 | tf_op jit(solution)/shard_map/psum | solution.py:116
  416.8 38.5 %psum.174 = f32[8]{0:T(128)S(1)} all-reduce(f32[8]{0:T(128)S(1)} %multiply_reduce_fusion.9), channel_id=1, replica_groups=mesh['lat'=4,'lon'=8] {'lat','lon'}, use_global_device_ids=true, to_apply=%region_32.0 | all-reduce | flops 8 | bytes 64 | tf_op jit(solution)/shard_map/psum | solution.py:146
  456.7 41.6 %psum.175 = f32[8]{0:T(128)S(1)} all-reduce(f32[8]{0:T(128)S(1)} %get-tuple-element.61), channel_id=1, replica_groups=mesh['lat'=4,'lon'=8] {'lat','lon'}, use_global_device_ids=true, to_apply=%region_34.0 | all-reduce | flops 8 | bytes 64 | tf_op jit(solution)/shard_map/psum | solution.py:149
  500.9 2.4 collective-permute-start.29
  503.3 6.8 collective-permute-done.28
  510.2 2.8 collective-permute-start.30
  521.9 38.7 %psum.176 = f32[8]{0:T(128)S(1)} all-reduce(f32[8]{0:T(128)S(1)} %copy-done.108), channel_id=1, replica_groups=mesh['lat'=4,'lon'=8] {'lat','lon'}, use_global_device_ids=true, to_apply=%region_36.0 | all-reduce | flops 8 | bytes 64 | tf_op jit(solution)/shard_map/psum | solution.py:146
  560.7 2.5 broadcast_multiply_fusion.4
  563.4 41.8 %psum.177 = f32[8]{0:T(128)S(1)} all-reduce(f32[8]{0:T(128)S(1)} %get-tuple-element.55), channel_id=1, replica_groups=mesh['lat'=4,'lon'=8] {'lat','lon'}, use_global_device_ids=true, to_apply=%region_38.0 | all-reduce | flops 8 | bytes 64 | tf_op jit(solution)/shard_map/psum | solution.py:149
  607.7 2.6 collective-permute-start.33
  610.3 6.7 collective-permute-done.32
  617.9 2.8 collective-permute-start.34
  625.6 2.8 multiply_reduce_fusion.5
  628.4 38.9 %psum.178 = f32[8]{0:T(128)} all-reduce(f32[8]{0:T(128)} %get-tuple-element.53), channel_id=1, replica_groups=mesh['lat'=4,'lon'=8] {'lat','lon'}, use_global_device_ids=true, to_apply=%region_40.0 | all-reduce | flops 8 | bytes 64 | tf_op jit(solution)/shard_map/psum | solution.py:146
  667.4 2.5 broadcast_multiply_fusion.3
  672.8 41.8 %psum.179 = f32[8]{0:T(128)S(1)} all-reduce(f32[8]{0:T(128)S(1)} %copy-done.107), channel_id=1, replica_groups=mesh['lat'=4,'lon'=8] {'lat','lon'}, use_global_device_ids=true, to_apply=%region_42.0 | all-reduce | flops 8 | bytes 64 | tf_op jit(solution)/shard_map/psum | solution.py:149
  718.2 2.5 collective-permute-start.37
  720.7 6.8 collective-permute-done.36
  728.3 3.4 collective-permute-start.38
  736.8 3.5 multiply_reduce_fusion.3
  741.1 38.3 %psum.180 = f32[8]{0:T(128)S(1)} all-reduce(f32[8]{0:T(128)S(1)} %copy-done.109), channel_id=1, replica_groups=mesh['lat'=4,'lon'=8] {'lat','lon'}, use_global_device_ids=true, to_apply=%region_44.0 | all-reduce | flops 8 | bytes 64 | tf_op jit(solution)/shard_map/psum | solution.py:146
  779.3 2.4 broadcast_multiply_fusion.2
  783.9 41.5 %psum.181 = f32[8]{0:T(128)S(1)} all-reduce(f32[8]{0:T(128)S(1)} %get-tuple-element.43), channel_id=1, replica_groups=mesh['lat'=4,'lon'=8] {'lat','lon'}, use_global_device_ids=true, to_apply=%region_46.0 | all-reduce | flops 8 | bytes 64 | tf_op jit(solution)/shard_map/psum | solution.py:149
  829.0 2.4 collective-permute-start.41
  831.4 6.7 collective-permute-done.40
  839.0 3.4 collective-permute-start.42
  848.2 3.6 multiply_reduce_fusion.1
  851.8 39.1 %psum.182 = f32[8]{0:T(128)} all-reduce(f32[8]{0:T(128)} %get-tuple-element.41), channel_id=1, replica_groups=mesh['lat'=4,'lon'=8] {'lat','lon'}, use_global_device_ids=true, to_apply=%region_48.0 | all-reduce | flops 8 | bytes 64 | tf_op jit(solution)/shard_map/psum | solution.py:146
  890.9 2.5 broadcast_multiply_fusion.1
  893.4 2.7 multiply_reduce_fusion
  896.1 42.2 %psum.183 = f32[8]{0:T(128)} all-reduce(f32[8]{0:T(128)} %get-tuple-element.37), channel_id=1, replica_groups=mesh['lat'=4,'lon'=8] {'lat','lon'}, use_global_device_ids=true, to_apply=%region_50.0 | all-reduce | flops 8 | bytes 64 | tf_op jit(solution)/shard_map/psum | solution.py:149
  942.1 2.5 collective-permute-start.45
  944.7 6.8 collective-permute-done.44
  951.6 2.8 collective-permute-start.46
  956.1 3.0 collective-permute-done.47
  961.3 3.9 collective-permute-start.49
  967.5 5.4 collective-permute-done.48
  976.4 2.5 fusion.51
  (356 shorter events, 88.8 us)
Async XLA Ops:
  1.7 2.2 collective-permute-start
  2.2 5.8 collective-permute-start.1
  8.1 5.3 collective-permute-start.2
  9.4 4.7 collective-permute-start.3
  16.1 502.2 %copy-start.18 = (f32[64,256]{1,0:T(8,128)}, f32[64,256]{1,0:T(8,128)S(1)}, u32[]{:S(2)}) copy-start(f32[64,256]{1,0:T(8,128)S(1)} %get-tuple-element.138) | copy-start | bytes 196612
  16.1 502.2 %copy-start.20 = (f32[64,256]{1,0:T(8,128)}, f32[64,256]{1,0:T(8,128)S(1)}, u32[]{:S(2)}) copy-start(f32[64,256]{1,0:T(8,128)S(1)} %get-tuple-element.139) | copy-start | bytes 196612
  16.1 502.2 %copy-start.22 = (f32[64,256]{1,0:T(8,128)}, f32[64,256]{1,0:T(8,128)S(1)}, u32[]{:S(2)}) copy-start(f32[64,256]{1,0:T(8,128)S(1)} %get-tuple-element.140) | copy-start | bytes 196612
  16.1 502.2 %copy-start.24 = (f32[64,256]{1,0:T(8,128)}, f32[64,256]{1,0:T(8,128)S(1)}, u32[]{:S(2)}) copy-start(f32[64,256]{1,0:T(8,128)S(1)} %get-tuple-element.141) | copy-start | bytes 196612
  16.2 5.1 collective-permute-start.4
  16.2 5.1 collective-permute-start.5
  21.4 345.6 %copy-start.61 = (f32[64,1]{1,0:T(8,128)}, f32[64,1]{1,0:T(8,128)S(1)}, u32[]{:S(2)}) copy-start(f32[64,1]{1,0:T(8,128)S(1)} %collective-permute-done.4) | copy-start | bytes 772
  21.4 345.6 %copy-start.63 = (f32[64,1]{1,0:T(8,128)}, f32[64,1]{1,0:T(8,128)S(1)}, u32[]{:S(2)}) copy-start(f32[64,1]{1,0:T(8,128)S(1)} %collective-permute-done.5) | copy-start | bytes 772
  21.5 4.9 collective-permute-start.6
  25.1 4.9 collective-permute-start.7
  30.8 102.2 %copy-start.34 = (f32[64,256]{1,0:T(8,128)}, f32[64,256]{1,0:T(8,128)S(1)}, u32[]{:S(2)}) copy-start(f32[64,256]{1,0:T(8,128)S(1)} %get-tuple-element.91) | copy-start | bytes 196612
  73.4 5.7 collective-permute-start.8
  76.3 2.7 collective-permute-start.9
  79.1 4.5 collective-permute-start.10
  82.3 4.3 collective-permute-start.11
  133.1 5.7 collective-permute-start.12
  136.0 2.8 collective-permute-start.13
  138.8 4.4 collective-permute-start.14
  141.9 4.3 collective-permute-start.15
  192.0 5.6 collective-permute-start.16
  194.8 2.8 collective-permute-start.17
  197.6 4.5 collective-permute-start.18
  200.8 4.3 collective-permute-start.19
  250.7 312.5 %copy-start.14 = (f32[64,256]{1,0:T(8,128)}, f32[64,256]{1,0:T(8,128)S(1)}, u32[]{:S(2)}) copy-start(f32[64,256]{1,0:T(8,128)S(1)} %get-tuple-element.77) | copy-start | bytes 196612
  250.7 312.5 %copy-start.50 = (f32[64,256]{1,0:T(8,128)}, f32[64,256]{1,0:T(8,128)S(1)}, u32[]{:S(2)}) copy-start(f32[64,256]{1,0:T(8,128)S(1)} %get-tuple-element.79) | copy-start | bytes 196612
  250.7 5.7 collective-permute-start.20
  253.7 2.8 collective-permute-start.21
  256.6 4.3 collective-permute-start.22
  259.6 4.3 collective-permute-start.23
  309.3 147.1 %copy-start.16 = (f32[64,256]{1,0:T(8,128)}, f32[64,256]{1,0:T(8,128)S(1)}, u32[]{:S(2)}) copy-start(f32[64,256]{1,0:T(8,128)S(1)} %get-tuple-element.73) | copy-start | bytes 196612
  309.3 147.1 %copy-start.52 = (f32[64,256]{1,0:T(8,128)}, f32[64,256]{1,0:T(8,128)S(1)}, u32[]{:S(2)}) copy-start(f32[64,256]{1,0:T(8,128)S(1)} %get-tuple-element.75) | copy-start | bytes 196612
  309.4 5.7 collective-permute-start.24
  312.2 2.8 collective-permute-start.25
  315.1 5.0 collective-permute-start.26
  318.2 4.3 collective-permute-start.27
  412.6 85.7 %copy-start.84 = (f32[6,8]{1,0:T(8,128)}, f32[6,8]{1,0:T(8,128)S(1)}, u32[]{:S(2)}) copy-start(f32[6,8]{1,0:T(8,128)S(1)} %get-tuple-element.21) | copy-start | bytes 580
  415.4 103.0 %copy-start.36 = (f32[64,256]{1,0:T(8,128)}, f32[64,256]{1,0:T(8,128)S(1)}, u32[]{:S(2)}) copy-start(f32[64,256]{1,0:T(8,128)S(1)} %multiply_add_fusion.12) | copy-start | bytes 196612
  499.7 10.4 %collective-permute-start.28 = (f32[8,64,1]{2,1,0:T(8,128)S(1)}, f32[8,64,1]{2,1,0:T(8,128)S(1)}, u32[]{:S(2)}, u32[]{:S(2)}) collective-permute-start(f32[8,64,1]{2,1,0:T(8,128)S(1)} %get-tuple-element.114), channel_id=1, source_target_pairs={{1,0},{2,1},{3,2},{4,3},{5,4},{6,5},{7,6},{0,7},{9,8},{10,9},{11,1... | collective-permute-start | bytes 6152 | tf_op jit(solution)/shard_map/ppermute | solution.py:19
  500.9 9.1 collective-permute-start.29
  510.2 6.5 collective-permute-start.30
  513.0 4.8 collective-permute-start.31
  606.7 10.3 %collective-permute-start.32 = (f32[8,64,1]{2,1,0:T(8,128)S(1)}, f32[8,64,1]{2,1,0:T(8,128)S(1)}, u32[]{:S(2)}, u32[]{:S(2)}) collective-permute-start(f32[8,64,1]{2,1,0:T(8,128)S(1)} %get-tuple-element.112), channel_id=1, source_target_pairs={{1,0},{2,1},{3,2},{4,3},{5,4},{6,5},{7,6},{0,7},{9,8},{10,9},{11,1... | collective-permute-start | bytes 6152 | tf_op jit(solution)/shard_map/ppermute | solution.py:19
  607.7 9.3 collective-permute-start.33
  617.9 6.6 collective-permute-start.34
  620.7 5.0 collective-permute-start.35
  628.4 108.4 %copy-start.1 = (f32[8,64,256]{2,1,0:T(8,128)}, f32[8,64,256]{2,1,0:T(8,128)S(1)}, u32[]{:S(2)}) copy-start(f32[8,64,256]{2,1,0:T(8,128)S(1)} %get-tuple-element.54) | copy-start | bytes 1572868
  717.1 10.4 %collective-permute-start.36 = (f32[8,64,1]{2,1,0:T(8,128)S(1)}, f32[8,64,1]{2,1,0:T(8,128)S(1)}, u32[]{:S(2)}, u32[]{:S(2)}) collective-permute-start(f32[8,64,1]{2,1,0:T(8,128)S(1)} %get-tuple-element.110), channel_id=1, source_target_pairs={{1,0},{2,1},{3,2},{4,3},{5,4},{6,5},{7,6},{0,7},{9,8},{10,9},{11,1... | collective-permute-start | bytes 6152 | tf_op jit(solution)/shard_map/ppermute | solution.py:19
  718.2 9.3 collective-permute-start.37
  728.3 7.2 collective-permute-start.38
  731.7 5.1 collective-permute-start.39
  827.8 10.3 %collective-permute-start.40 = (f32[8,64,1]{2,1,0:T(8,128)S(1)}, f32[8,64,1]{2,1,0:T(8,128)S(1)}, u32[]{:S(2)}, u32[]{:S(2)}) collective-permute-start(f32[8,64,1]{2,1,0:T(8,128)S(1)} %get-tuple-element.108), channel_id=1, source_target_pairs={{1,0},{2,1},{3,2},{4,3},{5,4},{6,5},{7,6},{0,7},{9,8},{10,9},{11,1... | collective-permute-start | bytes 6152 | tf_op jit(solution)/shard_map/ppermute | solution.py:19
  829.0 9.2 collective-permute-start.41
  839.0 9.1 collective-permute-start.42
  842.4 5.7 collective-permute-start.43
  941.1 10.4 %collective-permute-start.44 = (f32[8,64,1]{2,1,0:T(8,128)S(1)}, f32[8,64,1]{2,1,0:T(8,128)S(1)}, u32[]{:S(2)}, u32[]{:S(2)}) collective-permute-start(f32[8,64,1]{2,1,0:T(8,128)S(1)} %get-tuple-element.106), channel_id=1, source_target_pairs={{1,0},{2,1},{3,2},{4,3},{5,4},{6,5},{7,6},{0,7},{9,8},{10,9},{11,1... | collective-permute-start | bytes 6152 | tf_op jit(solution)/shard_map/ppermute | solution.py:19
  942.1 9.3 collective-permute-start.45
  951.6 4.5 collective-permute-start.46
  954.5 4.6 collective-permute-start.47
  961.3 14.4 %collective-permute-start.49 = (f32[8,1,256]{2,1,0:T(1,128)S(1)}, f32[8,1,256]{2,1,0:T(1,128)S(1)}, u32[]{:S(2)}, u32[]{:S(2)}) collective-permute-start(f32[8,1,256]{2,1,0:T(1,128)S(1)} %slice.651), channel_id=1, source_target_pairs={{8,0},{16,8},{24,16},{9,1},{17,9},{25,17},{10,2},{18,10},{26,18},{... | collective-permute-start | bytes 24584 | tf_op jit(solution)/shard_map/ppermute | solution.py:33
  965.1 7.8 collective-permute-start.48
  (96 other events, 1051.9 us)
where the time goes:
time: 984 us; the launch traced here: 979 us
  blocking collectives  691 us (70%)
  starting transfers between devices  102 us (10%)
  waiting for transfers between devices  79.1 us (8%)
  other arithmetic  58.4 us (6%)
  between operations  37.4 us (4%)
  local copies, waits for them, and re-layouts  11.5 us (1%)
    psum x6, blocking collectives, smoothed_terms(): lax.psum((jnp.sum(residual * precond), jnp.sum(precond * smooth)), ('lat'...  246 us
    psum x5, blocking collectives, body(): lax.psum(jnp.sum(res_new * image, axis=(1, 2)), ('lat', 'lon'))  209 us
    psum x5, blocking collectives, body(): lax.psum(jnp.sum(dir_bar * inner_dir, axis=(1, 2)), ('lat', 'lon'))  193 us
    ppermute x24, starting transfers between devices, padded_2(): lax.ppermute(lax.slice_in_dim(block, 0, width, axis=dim), axis, backward)  58.6 us
    ppermute x24, waiting for transfers between devices, padded_2(): lax.ppermute(lax.slice_in_dim(block, 0, width, axis=dim), axis, backward)  48 us
    psum x1, blocking collectives, body(): lax.psum(jnp.stack([jnp.sum(cost_weights * padded_dirs[step][1:-1, 1:-1],...  42.2 us
    ppermute x24, starting transfers between devices, padded_2(): lax.ppermute(lax.slice_in_dim(block, block.shape[dim] - width, None, axis...  38.3 us
    ppermute x24, waiting for transfers between devices, padded_2(): lax.ppermute(lax.slice_in_dim(block, block.shape[dim] - width, None, axis...  25.6 us
  transfers between devices with their start and end apart: 50, of which 25 were waited for; matrix products, arithmetic and copies ran while one was open for 0% of the time, Pallas kernels for 0%

commit v1 on v0

--- a/solution.py
+++ b/solution.py
@@ -64,9 +64,11 @@
     precond = residual / diagonal
     prec_pad = widen_precond(precond)
     smooth = operate(prec_pad, coefs)
-    norm_value, delta = lax.psum(
-        (jnp.sum(residual * precond), jnp.sum(precond * smooth)), ("lat", "lon")
-    )
+
+    def sheets_manage(tile_in):
+        return jax.lax.psum(jax.lax.psum(tile_in, "lat"), "lon")
+
+    norm_value, delta = sheets_manage((jnp.sum(residual * precond), jnp.sum(precond * smooth)))
     return (prec_pad, smooth, norm_value, delta)
 
 

time: 984 us -> 882 us (0.90)
  blocking collectives: 691 us -> 600 us
    psum x6 -> x12, blocking collectives: 246 us -> 155 us  [sheets_manage(): return jax.lax.psum(jax.lax.psum(tile_in, 'lat'), 'lon')]
    ppermute x24, starting transfers between devices: 58.6 us -> 37.5 us  [padded_2(): lax.ppermute(lax.slice_in_dim(block, 0, width, axis=dim), axis, backward)]
    ppermute x24, starting transfers between devices: 38.3 us -> 52.6 us  [padded_2(): lax.ppermute(lax.slice_in_dim(block, block.shape[dim] - width, None, axis...]
  transfers between devices with their start and end apart: 50 -> 50, of which waited for: 25 -> 24; matrix products, arithmetic and copies ran while one was open for 0% -> 0% of each run, Pallas kernels for 0% -> 0%
where the time goes in v1:
time: 882 us; the launch traced here: 879 us
  blocking collectives  600 us (68%)
  starting transfers between devices  95.2 us (11%)
  waiting for transfers between devices  77.2 us (9%)
  other arithmetic  55.2 us (6%)
  between operations  38.9 us (4%)
  local copies, waits for them, and re-layouts  12.8 us (1%)
    psum x5, blocking collectives, body(): lax.psum(jnp.sum(res_new * image, axis=(1, 2)), ('lat', 'lon'))  205 us
    psum x5, blocking collectives, body(): lax.psum(jnp.sum(dir_bar * inner_dir, axis=(1, 2)), ('lat', 'lon'))  200 us
    psum x12, blocking collectives, sheets_manage(): return jax.lax.psum(jax.lax.psum(tile_in, 'lat'), 'lon')  155 us
    ppermute x24, starting transfers between devices, padded_2(): lax.ppermute(lax.slice_in_dim(block, block.shape[dim] - width, None, axis...  52.6 us
    ppermute x24, waiting for transfers between devices, padded_2(): lax.ppermute(lax.slice_in_dim(block, 0, width, axis=dim), axis, backward)  46.3 us
    psum x1, blocking collectives, body(): lax.psum(jnp.stack([jnp.sum(cost_weights * padded_dirs[step][1:-1, 1:-1],...  39.1 us
    ppermute x24, starting transfers between devices, padded_2(): lax.ppermute(lax.slice_in_dim(block, 0, width, axis=dim), axis, backward)  37.5 us
    ppermute x24, waiting for transfers between devices, padded_2(): lax.ppermute(lax.slice_in_dim(block, block.shape[dim] - width, None, axis...  25.5 us
  transfers between devices with their start and end apart: 50, of which 24 were waited for; matrix products, arithmetic and copies ran while one was open for 0% of the time, Pallas kernels for 0%

profile of v1, /device:TPU:31, one launch (start us, length us, event | category | flops | bytes accessed | tf_op | source)
XLA Modules:
  0.0 878.8 jit_solution(13837184558350917533)
XLA Ops:
  3.8 4.2 collective-permute-done.1
  9.4 4.0 collective-permute-start.3
  16.2 3.5 collective-permute-start.5
  21.4 3.6 collective-permute-start.6
  26.4 3.6 collective-permute-done.7
  30.8 8.6 all-reduce.11
  39.4 17.2 %all-reduce.5 = (f32[]{:T(128)}, f32[]{:T(128)}) all-reduce(f32[]{:T(128)} %get-tuple-element.43, f32[]{:T(128)} %get-tuple-element.44), channel_id=1, replica_groups=mesh['lat'=4,'lon'=8] {'lon'}, use_global_device_ids=true, to_apply=%region_2.0 | all-reduce | flops 2 | bytes 16 | tf_op jit(solution)/shard_map/psum | solution.py:69
  58.0 4.1 collective-permute-start.9
  66.8 3.3 collective-permute-done.11
  70.9 8.6 all-reduce.10
  79.5 17.2 %all-reduce.4 = (f32[]{:T(128)}, f32[]{:T(128)}) all-reduce(f32[]{:T(128)} %get-tuple-element.41, f32[]{:T(128)} %get-tuple-element.42), channel_id=1, replica_groups=mesh['lat'=4,'lon'=8] {'lon'}, use_global_device_ids=true, to_apply=%region_8.0 | all-reduce | flops 2 | bytes 16 | tf_op jit(solution)/shard_map/psum | solution.py:69
  101.5 4.1 collective-permute-start.13
  110.2 3.3 collective-permute-done.15
  114.3 8.6 all-reduce.9
  123.0 17.3 %all-reduce.3 = (f32[]{:T(128)}, f32[]{:T(128)}) all-reduce(f32[]{:T(128)} %get-tuple-element.39, f32[]{:T(128)} %get-tuple-element.40), channel_id=1, replica_groups=mesh['lat'=4,'lon'=8] {'lon'}, use_global_device_ids=true, to_apply=%region_14.0 | all-reduce | flops 2 | bytes 16 | tf_op jit(solution)/shard_map/psum | solution.py:69
  144.5 4.1 collective-permute-start.17
  153.2 3.3 collective-permute-done.19
  157.3 8.6 all-reduce.8
  165.9 17.2 %all-reduce.2 = (f32[]{:T(128)}, f32[]{:T(128)}) all-reduce(f32[]{:T(128)} %get-tuple-element.37, f32[]{:T(128)} %get-tuple-element.38), channel_id=1, replica_groups=mesh['lat'=4,'lon'=8] {'lon'}, use_global_device_ids=true, to_apply=%region_20.0 | all-reduce | flops 2 | bytes 16 | tf_op jit(solution)/shard_map/psum | solution.py:69
  187.3 4.1 collective-permute-start.21
  196.0 3.3 collective-permute-done.23
  200.1 8.6 all-reduce.7
  208.7 17.2 %all-reduce.1 = (f32[]{:T(128)}, f32[]{:T(128)}) all-reduce(f32[]{:T(128)} %get-tuple-element.35, f32[]{:T(128)} %get-tuple-element.36), channel_id=1, replica_groups=mesh['lat'=4,'lon'=8] {'lon'}, use_global_device_ids=true, to_apply=%region_26.0 | all-reduce | flops 2 | bytes 16 | tf_op jit(solution)/shard_map/psum | solution.py:69
  229.9 4.1 collective-permute-start.25
  239.2 2.7 collective-permute-done.27
  242.7 8.6 all-reduce.6
  251.3 17.2 %all-reduce = (f32[]{:T(128)}, f32[]{:T(128)}) all-reduce(f32[]{:T(128)} %get-tuple-element.33, f32[]{:T(128)} %get-tuple-element.34), channel_id=1, replica_groups=mesh['lat'=4,'lon'=8] {'lon'}, use_global_device_ids=true, to_apply=%region_32.0 | all-reduce | flops 2 | bytes 16 | tf_op jit(solution)/shard_map/psum | solution.py:69
  276.8 39.1 %psum.269 = f32[6,8]{1,0:T(8,128)S(1)} all-reduce(f32[6,8]{1,0:T(8,128)S(1)} %stack.43), channel_id=1, replica_groups=mesh['lat'=4,'lon'=8] {'lat','lon'}, use_global_device_ids=true, to_apply=%region_42.0 | all-reduce | flops 48 | bytes 384 | tf_op jit(solution)/shard_map/psum | solution.py:118
  318.1 40.7 %psum.270 = f32[8]{0:T(128)S(1)} all-reduce(f32[8]{0:T(128)S(1)} %multiply_reduce_fusion.9), channel_id=1, replica_groups=mesh['lat'=4,'lon'=8] {'lat','lon'}, use_global_device_ids=true, to_apply=%region_44.0 | all-reduce | flops 8 | bytes 64 | tf_op jit(solution)/shard_map/psum | solution.py:148
  360.3 39.2 %psum.271 = f32[8]{0:T(128)S(1)} all-reduce(f32[8]{0:T(128)S(1)} %get-tuple-element.73), channel_id=1, replica_groups=mesh['lat'=4,'lon'=8] {'lat','lon'}, use_global_device_ids=true, to_apply=%region_46.0 | all-reduce | flops 8 | bytes 64 | tf_op jit(solution)/shard_map/psum | solution.py:151
  404.4 5.4 collective-permute-done.28
  409.9 2.8 collective-permute-start.30
  418.4 2.2 multiply_reduce_fusion.7
  421.1 41.8 %psum.272 = f32[8]{0:T(128)S(1)} all-reduce(f32[8]{0:T(128)S(1)} %copy-done.109), channel_id=1, replica_groups=mesh['lat'=4,'lon'=8] {'lat','lon'}, use_global_device_ids=true, to_apply=%region_48.0 | all-reduce | flops 8 | bytes 64 | tf_op jit(solution)/shard_map/psum | solution.py:148
  465.1 41.1 %psum.273 = f32[8]{0:T(128)S(1)} all-reduce(f32[8]{0:T(128)S(1)} %get-tuple-element.67), channel_id=1, replica_groups=mesh['lat'=4,'lon'=8] {'lat','lon'}, use_global_device_ids=true, to_apply=%region_50.0 | all-reduce | flops 8 | bytes 64 | tf_op jit(solution)/shard_map/psum | solution.py:151
  508.4 2.6 collective-permute-start.33
  511.1 6.4 collective-permute-done.32
  518.3 2.9 collective-permute-start.34
  525.7 2.7 multiply_reduce_fusion.5
  528.4 40.2 %psum.274 = f32[8]{0:T(128)} all-reduce(f32[8]{0:T(128)} %get-tuple-element.65), channel_id=1, replica_groups=mesh['lat'=4,'lon'=8] {'lat','lon'}, use_global_device_ids=true, to_apply=%region_52.0 | all-reduce | flops 8 | bytes 64 | tf_op jit(solution)/shard_map/psum | solution.py:148
  568.6 2.5 broadcast_multiply_fusion.3
  571.2 2.3 multiply_reduce_fusion.4
  574.1 41.3 %psum.275 = f32[8]{0:T(128)S(1)} all-reduce(f32[8]{0:T(128)S(1)} %copy-done.108), channel_id=1, replica_groups=mesh['lat'=4,'lon'=8] {'lat','lon'}, use_global_device_ids=true, to_apply=%region_54.0 | all-reduce | flops 8 | bytes 64 | tf_op jit(solution)/shard_map/psum | solution.py:151
  618.8 2.5 collective-permute-start.37
  621.3 6.8 collective-permute-done.36
  628.8 3.4 collective-permute-start.38
  637.4 3.5 multiply_reduce_fusion.3
  641.6 38.3 %psum.276 = f32[8]{0:T(128)S(1)} all-reduce(f32[8]{0:T(128)S(1)} %copy-done.110), channel_id=1, replica_groups=mesh['lat'=4,'lon'=8] {'lat','lon'}, use_global_device_ids=true, to_apply=%region_56.0 | all-reduce | flops 8 | bytes 64 | tf_op jit(solution)/shard_map/psum | solution.py:148
  683.9 41.5 %psum.277 = f32[8]{0:T(128)S(1)} all-reduce(f32[8]{0:T(128)S(1)} %get-tuple-element.55), channel_id=1, replica_groups=mesh['lat'=4,'lon'=8] {'lat','lon'}, use_global_device_ids=true, to_apply=%region_58.0 | all-reduce | flops 8 | bytes 64 | tf_op jit(solution)/shard_map/psum | solution.py:151
  728.9 2.4 collective-permute-start.41
  731.4 6.7 collective-permute-done.40
  738.9 3.4 collective-permute-start.42
  748.2 3.5 multiply_reduce_fusion.1
  751.8 38.9 %psum.278 = f32[8]{0:T(128)} all-reduce(f32[8]{0:T(128)} %get-tuple-element.53), channel_id=1, replica_groups=mesh['lat'=4,'lon'=8] {'lat','lon'}, use_global_device_ids=true, to_apply=%region_60.0 | all-reduce | flops 8 | bytes 64 | tf_op jit(solution)/shard_map/psum | solution.py:148
  790.7 2.6 broadcast_multiply_fusion.1
  793.3 2.7 multiply_reduce_fusion
  796.0 42.2 %psum.279 = f32[8]{0:T(128)} all-reduce(f32[8]{0:T(128)} %get-tuple-element.49), channel_id=1, replica_groups=mesh['lat'=4,'lon'=8] {'lat','lon'}, use_global_device_ids=true, to_apply=%region_62.0 | all-reduce | flops 8 | bytes 64 | tf_op jit(solution)/shard_map/psum | solution.py:151
  842.1 2.5 collective-permute-start.45
  844.6 6.8 collective-permute-done.44
  851.5 2.8 collective-permute-start.46
  856.2 2.7 collective-permute-done.47
  861.2 3.9 collective-permute-start.49
  867.5 5.4 collective-permute-done.48
  876.3 2.5 fusion.51
  (364 shorter events, 90.8 us)
Async XLA Ops:
  1.7 2.2 collective-permute-start
  2.2 5.8 collective-permute-start.1
  8.1 5.3 collective-permute-start.2
  9.4 4.7 collective-permute-start.3
  16.1 401.6 %copy-start.18 = (f32[64,256]{1,0:T(8,128)}, f32[64,256]{1,0:T(8,128)S(1)}, u32[]{:S(2)}) copy-start(f32[64,256]{1,0:T(8,128)S(1)} %get-tuple-element.150) | copy-start | bytes 196612
  16.1 401.6 %copy-start.20 = (f32[64,256]{1,0:T(8,128)}, f32[64,256]{1,0:T(8,128)S(1)}, u32[]{:S(2)}) copy-start(f32[64,256]{1,0:T(8,128)S(1)} %get-tuple-element.151) | copy-start | bytes 196612
  16.1 401.6 %copy-start.22 = (f32[64,256]{1,0:T(8,128)}, f32[64,256]{1,0:T(8,128)S(1)}, u32[]{:S(2)}) copy-start(f32[64,256]{1,0:T(8,128)S(1)} %get-tuple-element.152) | copy-start | bytes 196612
  16.1 401.6 %copy-start.24 = (f32[64,256]{1,0:T(8,128)}, f32[64,256]{1,0:T(8,128)S(1)}, u32[]{:S(2)}) copy-start(f32[64,256]{1,0:T(8,128)S(1)} %get-tuple-element.153) | copy-start | bytes 196612
  16.2 5.1 collective-permute-start.4
  16.2 5.1 collective-permute-start.5
  21.4 251.9 %copy-start.61 = (f32[64,1]{1,0:T(8,128)}, f32[64,1]{1,0:T(8,128)S(1)}, u32[]{:S(2)}) copy-start(f32[64,1]{1,0:T(8,128)S(1)} %collective-permute-done.4) | copy-start | bytes 772
  21.4 251.9 %copy-start.63 = (f32[64,1]{1,0:T(8,128)}, f32[64,1]{1,0:T(8,128)S(1)}, u32[]{:S(2)}) copy-start(f32[64,1]{1,0:T(8,128)S(1)} %collective-permute-done.5) | copy-start | bytes 772
  21.4 4.9 collective-permute-start.6
  25.1 4.9 collective-permute-start.7
  26.4 246.9 %copy-start.80 = (f32[1,258]{1,0:T(1,128)}, f32[1,258]{1,0:T(1,128)S(1)}, u32[]{:S(2)}) copy-start(f32[1,258]{1,0:T(1,128)S(1)} %collective-permute-done.6) | copy-start | bytes 3100
  30.8 70.6 %copy-start.34 = (f32[64,256]{1,0:T(8,128)}, f32[64,256]{1,0:T(8,128)S(1)}, u32[]{:S(2)}) copy-start(f32[64,256]{1,0:T(8,128)S(1)} %get-tuple-element.103) | copy-start | bytes 196612
  58.0 5.7 collective-permute-start.8
  58.0 5.7 collective-permute-start.9
  63.8 3.0 collective-permute-start.10
  65.5 4.6 collective-permute-start.11
  101.5 5.7 collective-permute-start.12
  101.5 5.7 collective-permute-start.13
  107.3 3.0 collective-permute-start.14
  108.9 4.6 collective-permute-start.15
  144.5 5.7 collective-permute-start.16
  144.5 5.7 collective-permute-start.17
  150.2 3.0 collective-permute-start.18
  151.9 4.6 collective-permute-start.19
  187.2 277.6 %copy-start.14 = (f32[64,256]{1,0:T(8,128)}, f32[64,256]{1,0:T(8,128)S(1)}, u32[]{:S(2)}) copy-start(f32[64,256]{1,0:T(8,128)S(1)} %get-tuple-element.89) | copy-start | bytes 196612
  187.2 277.6 %copy-start.50 = (f32[64,256]{1,0:T(8,128)}, f32[64,256]{1,0:T(8,128)S(1)}, u32[]{:S(2)}) copy-start(f32[64,256]{1,0:T(8,128)S(1)} %get-tuple-element.91) | copy-start | bytes 196612
  187.2 5.7 collective-permute-start.20
  187.3 5.7 collective-permute-start.21
  193.0 3.0 collective-permute-start.22
  194.7 4.6 collective-permute-start.23
  229.8 130.2 %copy-start.16 = (f32[64,256]{1,0:T(8,128)}, f32[64,256]{1,0:T(8,128)S(1)}, u32[]{:S(2)}) copy-start(f32[64,256]{1,0:T(8,128)S(1)} %get-tuple-element.85) | copy-start | bytes 196612
  229.8 130.2 %copy-start.52 = (f32[64,256]{1,0:T(8,128)}, f32[64,256]{1,0:T(8,128)S(1)}, u32[]{:S(2)}) copy-start(f32[64,256]{1,0:T(8,128)S(1)} %get-tuple-element.87) | copy-start | bytes 196612
  229.9 5.7 collective-permute-start.24
  229.9 5.7 collective-permute-start.25
  235.6 3.6 collective-permute-start.26
  237.3 4.6 collective-permute-start.27
  316.7 101.1 %copy-start.36 = (f32[64,256]{1,0:T(8,128)}, f32[64,256]{1,0:T(8,128)S(1)}, u32[]{:S(2)}) copy-start(f32[64,256]{1,0:T(8,128)S(1)} %multiply_add_fusion.12) | copy-start | bytes 196612
  400.8 9.0 %collective-permute-start.28 = (f32[8,64,1]{2,1,0:T(8,128)S(1)}, f32[8,64,1]{2,1,0:T(8,128)S(1)}, u32[]{:S(2)}, u32[]{:S(2)}) collective-permute-start(f32[8,64,1]{2,1,0:T(8,128)S(1)} %get-tuple-element.126), channel_id=1, source_target_pairs={{1,0},{2,1},{3,2},{4,3},{5,4},{6,5},{7,6},{0,7},{9,8},{10,9},{11,1... | collective-permute-start | bytes 6152 | tf_op jit(solution)/shard_map/ppermute | solution.py:19
  402.4 7.4 collective-permute-start.29
  409.9 6.6 collective-permute-start.30
  412.7 4.4 collective-permute-start.31
  507.5 10.0 %collective-permute-start.32 = (f32[8,64,1]{2,1,0:T(8,128)S(1)}, f32[8,64,1]{2,1,0:T(8,128)S(1)}, u32[]{:S(2)}, u32[]{:S(2)}) collective-permute-start(f32[8,64,1]{2,1,0:T(8,128)S(1)} %get-tuple-element.124), channel_id=1, source_target_pairs={{1,0},{2,1},{3,2},{4,3},{5,4},{6,5},{7,6},{0,7},{9,8},{10,9},{11,1... | collective-permute-start | bytes 6152 | tf_op jit(solution)/shard_map/ppermute | solution.py:19
  508.4 9.0 %collective-permute-start.33 = (f32[8,64,1]{2,1,0:T(8,128)S(1)}, f32[8,64,1]{2,1,0:T(8,128)S(1)}, u32[]{:S(2)}, u32[]{:S(2)}) collective-permute-start(f32[8,64,1]{2,1,0:T(8,128)S(1)} %get-tuple-element.123), channel_id=1, source_target_pairs={{0,1},{1,2},{2,3},{3,4},{4,5},{5,6},{6,7},{7,0},{8,9},{9,10},{10,1... | collective-permute-start | bytes 6152 | tf_op jit(solution)/shard_map/ppermute | solution.py:16
  518.3 6.8 collective-permute-start.34
  521.2 4.5 collective-permute-start.35
  528.4 109.0 %copy-start.1 = (f32[8,64,256]{2,1,0:T(8,128)}, f32[8,64,256]{2,1,0:T(8,128)S(1)}, u32[]{:S(2)}) copy-start(f32[8,64,256]{2,1,0:T(8,128)S(1)} %get-tuple-element.66) | copy-start | bytes 1572868
  617.7 10.4 %collective-permute-start.36 = (f32[8,64,1]{2,1,0:T(8,128)S(1)}, f32[8,64,1]{2,1,0:T(8,128)S(1)}, u32[]{:S(2)}, u32[]{:S(2)}) collective-permute-start(f32[8,64,1]{2,1,0:T(8,128)S(1)} %get-tuple-element.122), channel_id=1, source_target_pairs={{1,0},{2,1},{3,2},{4,3},{5,4},{6,5},{7,6},{0,7},{9,8},{10,9},{11,1... | collective-permute-start | bytes 6152 | tf_op jit(solution)/shard_map/ppermute | solution.py:19
  618.8 9.3 %collective-permute-start.37 = (f32[8,64,1]{2,1,0:T(8,128)S(1)}, f32[8,64,1]{2,1,0:T(8,128)S(1)}, u32[]{:S(2)}, u32[]{:S(2)}) collective-permute-start(f32[8,64,1]{2,1,0:T(8,128)S(1)} %get-tuple-element.121), channel_id=1, source_target_pairs={{0,1},{1,2},{2,3},{3,4},{4,5},{5,6},{6,7},{7,0},{8,9},{9,10},{10,1... | collective-permute-start | bytes 6152 | tf_op jit(solution)/shard_map/ppermute | solution.py:16
  628.8 7.4 collective-permute-start.38
  632.3 5.1 collective-permute-start.39
  727.8 10.3 %collective-permute-start.40 = (f32[8,64,1]{2,1,0:T(8,128)S(1)}, f32[8,64,1]{2,1,0:T(8,128)S(1)}, u32[]{:S(2)}, u32[]{:S(2)}) collective-permute-start(f32[8,64,1]{2,1,0:T(8,128)S(1)} %get-tuple-element.120), channel_id=1, source_target_pairs={{1,0},{2,1},{3,2},{4,3},{5,4},{6,5},{7,6},{0,7},{9,8},{10,9},{11,1... | collective-permute-start | bytes 6152 | tf_op jit(solution)/shard_map/ppermute | solution.py:19
  728.9 9.2 %collective-permute-start.41 = (f32[8,64,1]{2,1,0:T(8,128)S(1)}, f32[8,64,1]{2,1,0:T(8,128)S(1)}, u32[]{:S(2)}, u32[]{:S(2)}) collective-permute-start(f32[8,64,1]{2,1,0:T(8,128)S(1)} %get-tuple-element.119), channel_id=1, source_target_pairs={{0,1},{1,2},{2,3},{3,4},{4,5},{5,6},{6,7},{7,0},{8,9},{9,10},{10,1... | collective-permute-start | bytes 6152 | tf_op jit(solution)/shard_map/ppermute | solution.py:16
  738.9 9.3 %collective-permute-start.42 = (f32[8,1,258]{2,1,0:T(1,128)}, f32[8,1,258]{2,1,0:T(1,128)}, u32[]{:S(2)}, u32[]{:S(2)}) collective-permute-start(f32[8,1,258]{2,1,0:T(1,128)} %get-tuple-element.109), channel_id=1, source_target_pairs={{8,0},{16,8},{24,16},{9,1},{17,9},{25,17},{10,2},{18,10},{26,18},{... | collective-permute-start | bytes 24776 | tf_op jit(solution)/shard_map/ppermute | solution.py:19
  742.3 5.9 collective-permute-start.43
  841.0 10.4 %collective-permute-start.44 = (f32[8,64,1]{2,1,0:T(8,128)S(1)}, f32[8,64,1]{2,1,0:T(8,128)S(1)}, u32[]{:S(2)}, u32[]{:S(2)}) collective-permute-start(f32[8,64,1]{2,1,0:T(8,128)S(1)} %get-tuple-element.118), channel_id=1, source_target_pairs={{1,0},{2,1},{3,2},{4,3},{5,4},{6,5},{7,6},{0,7},{9,8},{10,9},{11,1... | collective-permute-start | bytes 6152 | tf_op jit(solution)/shard_map/ppermute | solution.py:19
  842.1 9.3 %collective-permute-start.45 = (f32[8,64,1]{2,1,0:T(8,128)S(1)}, f32[8,64,1]{2,1,0:T(8,128)S(1)}, u32[]{:S(2)}, u32[]{:S(2)}) collective-permute-start(f32[8,64,1]{2,1,0:T(8,128)S(1)} %get-tuple-element.117), channel_id=1, source_target_pairs={{0,1},{1,2},{2,3},{3,4},{4,5},{5,6},{6,7},{7,0},{8,9},{9,10},{10,1... | collective-permute-start | bytes 6152 | tf_op jit(solution)/shard_map/ppermute | solution.py:16
  851.5 4.7 collective-permute-start.46
  854.4 4.6 collective-permute-start.47
  861.2 14.5 %collective-permute-start.49 = (f32[8,1,256]{2,1,0:T(1,128)S(1)}, f32[8,1,256]{2,1,0:T(1,128)S(1)}, u32[]{:S(2)}, u32[]{:S(2)}) collective-permute-start(f32[8,1,256]{2,1,0:T(1,128)S(1)} %slice.651), channel_id=1, source_target_pairs={{8,0},{16,8},{24,16},{9,1},{17,9},{25,17},{10,2},{18,10},{26,18},{... | collective-permute-start | bytes 24584 | tf_op jit(solution)/shard_map/ppermute | solution.py:33
  865.1 7.8 collective-permute-start.48
  (97 other events, 968.4 us)
